TPU v7x, 32 devices: a whole 2x2x4 slice. The times are simulated.
32 devices in a mesh: band: 8 (over y, x, core), chan: 4 (over z).
Axes of the slice: x: 2, y: 2, z: 4, core: 2. Of those that a mesh axis runs over, the one named last changes fastest.
Arguments:
- cells_next: bfloat16 [16384, 1024], P('band', 'chan'), may hold values from -6 to 6
- node_embed: bfloat16 [2048, 1024], P('band', 'chan'), may hold values from -6 to 6
- enc_mix: bfloat16 [1024, 1024], P(None, 'chan'), may hold values from -0.1875 to 0.1875
- out_cotangent: bfloat16 [16384, 1024], P('band', 'chan'), may hold values from -6 to 6
- decoded_saved: bfloat16 [16384, 1024], P('band', 'chan'), may hold values from -6 to 6
- dec_proj: bfloat16 [1024, 1024], P(None, 'chan'), may hold values from -0.1875 to 0.1875
- tile_source: int32 [16, 16], replicated, may hold values from 0 to 127, as said below
- tile_codes: int32 [16, 16, 128, 128], P('band'), may hold values from 0 to 65535
Outputs:
- hidden_nodes: bfloat16 [2048, 1024], P('band', 'chan')
- node_grad: bfloat16 [2048, 1024], P('band', 'chan')
- w_dec_grad: float32 [1024, 1024], P('band', 'chan')
Inputs may be any that keep to these rules, and one draw needn't show every extreme that they name: `tile_source`: each entry is a cell block; cell block c lies in band c // 16 and node block n in band n // 2. The cell blocks of a node block's tiles lie within 3 bands of its own. Of the 32 tiles of one band's node blocks, exactly 8 read that band itself and at most 8 read any other one band.
All inputs are finite; a program needn't handle non-finite values.
Results may differ from a plain program's by a relative error of at most 0.0049.
Values may be sent and summed in bfloat16 or wider, within the bound.
A program may use at most 64 MiB of HBM per device.

v0:
```python
import functools

import jax
import jax.numpy as jnp
from jax import lax
from jax.experimental import pallas as pl
from jax.experimental.pallas import tpu as pltpu
from jax.sharding import PartitionSpec as P

R = 3
CAP = 8
OFFS = [o for o in range(-R, R + 1) if o != 0]
SEND_ORDER = [3, -3, 2, -2, 1, -1]
SERVE_ORDER = [1, -1, 2, -2, 3, -3]
NCH = 4
KH = NCH // 2
CHUNKS = list(range(KH, NCH)) + list(range(KH))
MESH = pl.DeviceIdType.MESH
F32 = jnp.float32
BF16 = jnp.bfloat16


def tables_for(tile_source, me, nb, tiles, nodes, cb):
    rows = tile_source.reshape(nb, tiles)
    offs = jnp.arange(-R, R + 1, dtype=jnp.int32)
    served = rows[jnp.clip(me - offs, 0, nb - 1)]
    order = jnp.arange(tiles, dtype=jnp.int32)
    before = order[None, :] < order[:, None]

    def onehot(sel):
        rank = jnp.sum((sel[:, None, :] & before[None]).astype(jnp.int32), axis=2)
        slots = jnp.arange(CAP, dtype=jnp.int32)
        return (sel[:, :, None] & (rank[:, :, None] == slots)).astype(jnp.int32)

    serve = onehot(served // cb == me)
    blk = jnp.sum(serve * (served % cb)[:, :, None], axis=1)
    mask = jnp.sum(serve.reshape(2 * R + 1, nodes, tiles // nodes, CAP), axis=2)
    mine = rows[me]
    send = onehot((mine // cb)[None, :] == (me + offs)[:, None])
    tidx = jnp.sum(send * order[None, :, None], axis=1)
    return tidx, blk, mask.astype(F32)


def kernel(
    nb, n, scale, wscale,
    tidx, blk, msk, cells_in, embed, emix_in, cot_in, dsv_in, dproj_in, codes_in,
    hid, ngrad, wgrad,
    cells, emix, cot, dsv, dproj, codes, ls,
    buf, hbuf, hsend, hrecv, wacc, wsend, wrecv, qsend, qrecv, psend, precv, lhs, acc,
    asend, abuf,
    zs, zr, hs, hr, hps, hpr, ws, wr, qs, qr, ps, pr, zas, zar,
):
    me = lax.axis_index("band")
    c = lax.axis_index("chan")
    nodes = msk.shape[1]
    blkrows = cells.shape[1]
    ch = embed.shape[1]
    cb = cot.shape[0]
    krows = cb * blkrows
    cblk = cb // NCH
    half = krows // 2
    hblk = cb // 2
    wrows = wrecv.shape[1]
    per = ch // wrows

    def rc(src, dst, ss, rs, dev):
        return pltpu.make_async_remote_copy(
            src_ref=src, dst_ref=dst, send_sem=ss, recv_sem=rs, device_id=dev, device_id_type=MESH
        )

    pos = [c, n - 1 - c]
    nxt = [lax.rem(c + 1, n), lax.rem(c + n - 1, n)]
    prv = [nxt[1], nxt[0]]

    def owner(f, d):
        return c - 1 - d if f == 0 else c + 1 + d

    def z_sends(f, d, k):
        ok = (pos[f] + 1 < n) & (pos[f] - d >= 0)
        return ok if k >= KH else ok & (pos[f] + 1 < n - 1)

    def z_recvs(f, d, k):
        ok = pos[f] - 1 - d >= 0
        return ok if k >= KH else ok & (pos[f] < n - 1)

    def z_copy(f, d, k):
        rows = pl.ds(k * cblk, cblk)
        src = cot.at[rows] if d == 0 else buf.at[f, d - 1, rows]
        return rc(src, buf.at[f, d, rows], zs.at[f, d, k], zr.at[f, d, k], {"chan": nxt[f]})

    def a_sends(f, d):
        return (pos[f] + 1 < n) & (pos[f] - d >= 0)

    def a_recvs(f, d):
        return pos[f] - 1 - d >= 0

    def a_copy(f, d, t):
        src = asend.at[t] if d == 0 else abuf.at[f, d - 1, t]
        return rc(src, abuf.at[f, d, t], zas.at[f, d, t], zar.at[f, d, t], {"chan": nxt[f]})

    def help_copy(f):
        return rc(dsv.at[pl.ds(0, half)], hbuf.at[f], hs.at[f], hr.at[f], {"chan": prv[f]})

    def part_copy(f, e):
        return rc(hsend.at[f, e], hrecv.at[f, e], hps.at[f, e], hpr.at[f, e], {"chan": nxt[f]})

    def q_copy(o):
        i = OFFS.index(o)
        return rc(qsend.at[i], qrecv.at[i], qs.at[i], qr.at[i], {"band": lax.rem(me + o + nb, nb)})

    def p_copy(o):
        i = OFFS.index(o)
        return rc(psend.at[i], precv.at[i], ps.at[i], pr.at[i], {"band": lax.rem(me - o + nb, nb)})

    def q_sends(o):
        return (me + o >= 0) & (me + o < nb)

    def q_recvs(o):
        return (me - o >= 0) & (me - o < nb)

    def w_copy(s):
        rows = pl.ds(pl.multiple_of(s * wrows, wrows), wrows)
        return rc(wsend.at[rows], wrecv.at[me], ws.at[s], wr.at[me], {"band": s})

    def w_from(s):
        rows = pl.ds(pl.multiple_of(s * wrows, wrows), wrows)
        return rc(wsend.at[rows], wrecv.at[s], ws.at[s], wr.at[s], {"band": s})

    def wdot(a, b):
        a = a.reshape(-1, ch)
        return lax.dot_general(a, b, (((0,), (0,)), ((), ())), preferred_element_type=F32)

    def w_done(own):
        rows = pl.ds(pl.multiple_of(own * ch, ch), ch)
        wsend[rows, :] = wacc[rows, :].astype(BF16)

        @pl.loop(0, per)
        def _(j):
            s = own * per + j

            @pl.when(s != me)
            def _():
                w_copy(s).start()

    def w_add(own, value, first):
        rows = pl.ds(pl.multiple_of(own * ch, ch), ch)
        if first:
            wacc[rows, :] = value
        else:
            wacc[rows, :] += value

    loads = {
        name: pltpu.make_async_copy(src, dst, ls.at[i])
        for i, (name, src, dst) in enumerate(
            (
                ("cot", cot_in, cot),
                ("codes", codes_in, codes),
                ("dsv", dsv_in, dsv),
                ("cells", cells_in, cells),
                ("emix", emix_in, emix),
                ("dproj", dproj_in, dproj),
            )
        )
    }
    for load_in in loads.values():
        load_in.start()

    barrier = pltpu.get_barrier_semaphore()

    @pl.loop(1, nb)
    def _(j):
        pl.semaphore_signal(
            barrier, inc=1, device_id={"band": lax.rem(me + j, nb)}, device_id_type=MESH
        )

    for f in range(2):
        @pl.when(pos[f] + 1 < n)
        def _():
            pl.semaphore_signal(barrier, inc=1, device_id={"chan": nxt[f]}, device_id_type=MESH)

    beside = jnp.where(c > 0, 1, 0) + jnp.where(c < n - 1, 1, 0)
    pl.semaphore_wait(barrier, nb - 1 + beside)

    loads["cot"].wait()
    for k in CHUNKS[:KH]:
        for f in range(2):
            @pl.when(z_sends(f, 0, k))
            def _():
                z_copy(f, 0, k).start()
    for k in CHUNKS[KH:]:
        for f in range(2):
            @pl.when(z_sends(f, 0, k))
            def _():
                z_copy(f, 0, k).start()

    loads["codes"].wait()
    for o in SEND_ORDER:
        @pl.when(q_sends(o))
        def _():
            i = OFFS.index(o)
            for s in range(CAP):
                qsend[i, s] = (codes[tidx[o + R, s]] - 32768).astype(jnp.int16)
            q_copy(o).start()

    loads["dsv"].wait()
    for f in range(2):
        @pl.when(pos[f] == n - 1)
        def _():
            help_copy(f).start()

    loads["cells"].wait()

    def serve(o, load):
        for s in range(CAP):
            word = load(s)
            cols = pl.ds(s * blkrows, blkrows)
            enc = ((word & 255) - 128).astype(F32)
            dec = (word >> 8).astype(F32)
            for m in range(nodes):
                keep = msk[o + R, m, s]
                rows = pl.ds(m * blkrows, blkrows)
                lhs[0, rows, cols] = (enc * keep).astype(BF16)
                lhs[1, rows, cols] = (dec * keep).astype(BF16)
        out = []
        for t, src in enumerate((cells, cot)):
            rhs = [src[blk[o + R, s]] for s in range(CAP)]
            out.append(jnp.dot(lhs[t], jnp.concatenate(rhs, axis=0), preferred_element_type=F32))
        return out

    own = serve(0, lambda s: codes[tidx[R, s]] - 32768)
    acc[0], acc[1] = own

    w_add(c, wdot(cot[...], dsv[...]), True)
    w_done(c)

    def answer(o):
        @pl.when(q_recvs(o))
        def _():
            i = OFFS.index(o)
            q_copy(o).wait_recv()
            parts = serve(o, lambda s: qrecv[i, s].astype(jnp.int32))
            psend[i, 0] = parts[0].astype(BF16)
            psend[i, 1] = parts[1].astype(BF16)
            p_copy(o).start()

    def aggregate():
        for o in SERVE_ORDER:
            @pl.when(q_sends(o))
            def _():
                i = OFFS.index(o)
                p_copy(o).wait_recv()
                for t in range(2):
                    acc[t] += precv[i, t].astype(F32)
        for t in range(2):
            asend[t] = (acc[t] * scale).astype(BF16)
            for f in range(2):
                @pl.when(a_sends(f, 0))
                def _():
                    a_copy(f, 0, t).start()

    pending = list(SERVE_ORDER)
    for d in range(n - 1):
        for j, k in enumerate(CHUNKS):
            for f in range(2):
                @pl.when(z_recvs(f, d, k))
                def _():
                    z_copy(f, d, k).wait_recv()

                    if d + 1 < n - 1:
                        @pl.when(z_sends(f, d + 1, k))
                        def _():
                            z_copy(f, d + 1, k).start()
            for o in pending[:2]:
                answer(o)
            pending = pending[2:]
            if j == KH - 1:
                for f in range(2):
                    @pl.when(z_recvs(f, d, NCH - 1))
                    def _():
                        w_add(owner(f, d), wdot(buf[f, d, hblk:], dsv[half:]), True)
                if d == 1:
                    aggregate()
            if j == NCH - 1:
                for f in range(2):
                    if d == 0:
                        @pl.when(pos[f] == n - 2)
                        def _():
                            help_copy(f).wait_recv()
                            hsend[f, 0] = wdot(cot[:hblk], hbuf[f]).astype(BF16)
                            part_copy(f, 0).start()

                    @pl.when(z_recvs(f, d, 0))
                    def _():
                        if d + 1 < n - 1:
                            @pl.when(pos[f] == n - 2)
                            def _():
                                hsend[f, d + 1] = wdot(buf[f, d, :hblk], hbuf[f]).astype(BF16)
                                part_copy(f, d + 1).start()

                        w_add(owner(f, d), wdot(buf[f, d, :hblk], dsv[:half]), False)
                        w_done(owner(f, d))

    mixes = (emix, dproj)
    loads["emix"].wait()
    loads["dproj"].wait()

    def mix(t, own, value):
        rows = pl.ds(pl.multiple_of(own * ch, ch), ch)
        return jnp.dot(value, mixes[t][rows, :], preferred_element_type=F32)

    for t in range(2):
        acc[t] = mix(t, c, asend[t])

    for d in range(n - 1):
        for f in range(2):
            @pl.when(pos[f] == n - 1)
            def _():
                part_copy(f, d).wait_recv()
                w_add(owner(f, d), hrecv[f, d].astype(F32), False)
                w_done(owner(f, d))

    for d in range(n - 1):
        for t in range(2):
            for f in range(2):
                @pl.when(a_recvs(f, d))
                def _():
                    a_copy(f, d, t).wait_recv()
                    if d + 1 < n - 1:
                        @pl.when(a_sends(f, d + 1))
                        def _():
                            a_copy(f, d + 1, t).start()
                    acc[t] += mix(t, owner(f, d), abuf[f, d, t])

    mixed = acc[0]
    hid[...] = (embed[...].astype(F32) + mixed / (1.0 + jnp.exp(-mixed))).astype(BF16)
    ngrad[...] = acc[1].astype(BF16)

    wgrad[...] = wacc[pl.ds(pl.multiple_of(me * wrows, wrows), wrows), :]

    @pl.loop(0, nb)
    def _(s):
        @pl.when(s != me)
        def _():
            w_from(s).wait_recv()
            wgrad[...] += wrecv[s].astype(F32)

    wgrad[...] = wgrad[...] * wscale

    for f in range(2):
        for d in range(n - 1):
            for k in CHUNKS:
                @pl.when(z_sends(f, d, k))
                def _():
                    z_copy(f, d, k).wait_send()
            for t in range(2):
                @pl.when(a_sends(f, d))
                def _():
                    a_copy(f, d, t).wait_send()

            @pl.when(pos[f] == n - 2)
            def _():
                part_copy(f, d).wait_send()

        @pl.when(pos[f] == n - 1)
        def _():
            help_copy(f).wait_send()
    for o in OFFS:
        @pl.when(q_sends(o))
        def _():
            q_copy(o).wait_send()

        @pl.when(q_recvs(o))
        def _():
            p_copy(o).wait_send()

    @pl.loop(0, nb)
    def _(s):
        @pl.when(s != me)
        def _():
            w_copy(s).wait_send()


def hand_over(hid_in, ngrad_in, wgrad_in, hid, ngrad, wgrad):
    hid[...] = hid_in[...]
    ngrad[...] = ngrad_in[...]
    wgrad[...] = wgrad_in[...]


def shards(nb, n, cells_next, node_embed, enc_mix, out_cotangent, decoded_saved, dec_proj, tile_source, tile_codes):
    me = lax.axis_index("band")
    nodes, kk, blkn, blkc = tile_codes.shape
    tiles = nodes * kk
    krows, ch = out_cotangent.shape
    cb = krows // blkc
    width = enc_mix.shape[0]
    wrows = width // nb
    scale = (3.0 / (kk * blkn)) ** 0.5 / 128.0
    wscale = float(krows * nb) ** -0.5
    tidx, blk, msk = tables_for(tile_source, me, nb, tiles, nodes, cb)
    no = len(OFFS)
    nn = nodes * blkn
    dma = pltpu.SemaphoreType.DMA
    vm = pltpu.VMEM
    outs = pl.pallas_call(
        functools.partial(kernel, nb, n, scale, wscale),
        name="encode_and_grad",
        out_shape=(
            jax.ShapeDtypeStruct((nn, ch), BF16),
            jax.ShapeDtypeStruct((nn, ch), BF16),
            jax.ShapeDtypeStruct((wrows, ch), F32),
        ),
        in_specs=[pl.BlockSpec(memory_space=pltpu.SMEM)] * 3
        + [pl.BlockSpec(memory_space=pl.ANY), pl.BlockSpec(memory_space=vm)]
        + [pl.BlockSpec(memory_space=pl.ANY)] * 5,
        out_specs=[pl.BlockSpec(memory_space=vm)] * 3,
        scratch_shapes=[
            vm((cb, blkc, ch), BF16),
            vm((width, ch), BF16),
            vm((cb, blkc, ch), BF16),
            vm((krows, ch), BF16),
            vm((width, ch), BF16),
            vm((tiles, blkn, blkc), jnp.int32),
            dma((6,)),
            vm((2, n - 1, cb, blkc, ch), BF16),
            vm((2, krows // 2, ch), BF16),
            vm((2, n - 1, ch, ch), BF16),
            vm((2, n - 1, ch, ch), BF16),
            vm((width, ch), F32),
            vm((width, ch), BF16),
            vm((nb, wrows, ch), BF16),
            vm((no, CAP, blkn, blkc), jnp.int16),
            vm((no, CAP, blkn, blkc), jnp.int16),
            vm((no, 2, nn, ch), BF16),
            vm((no, 2, nn, ch), BF16),
            vm((2, nn, CAP * blkc), BF16),
            vm((2, nn, ch), F32),
            vm((2, nn, ch), BF16),
            vm((2, n - 1, 2, nn, ch), BF16),
            dma((2, n - 1, NCH)),
            dma((2, n - 1, NCH)),
            dma((2,)),
            dma((2,)),
            dma((2, n - 1)),
            dma((2, n - 1)),
            dma((nb,)),
            dma((nb,)),
            dma((no,)),
            dma((no,)),
            dma((no,)),
            dma((no,)),
            dma((2, n - 1, 2)),
            dma((2, n - 1, 2)),
        ],
        compiler_params=pltpu.CompilerParams(
            collective_id=0, has_side_effects=True, vmem_limit_bytes=56 * 1024 * 1024
        ),
    )(
        tidx, blk, msk,
        cells_next.reshape(cb, blkc, ch), node_embed, enc_mix,
        out_cotangent.reshape(cb, blkc, ch), decoded_saved, dec_proj,
        tile_codes.reshape(tiles, blkn, blkc),
    )
    return pl.pallas_call(
        hand_over,
        name="hand_over",
        out_shape=tuple(jax.ShapeDtypeStruct(x.shape, x.dtype) for x in outs),
        in_specs=[pl.BlockSpec(memory_space=vm)] * 3,
        out_specs=[pl.BlockSpec(memory_space=vm)] * 3,
    )(*outs)


def solution(mesh):
    nb, n = mesh.shape["band"], mesh.shape["chan"]
    in_specs = (
        P("band", "chan"),
        P("band", "chan"),
        P(None, "chan"),
        P("band", "chan"),
        P("band", "chan"),
        P(None, "chan"),
        P(),
        P("band", None, None, None),
    )
    out_specs = (P("band", "chan"), P("band", "chan"), P("band", "chan"))
    return jax.shard_map(
        functools.partial(shards, nb, n),
        mesh=mesh,
        in_specs=in_specs,
        out_specs=out_specs,
        check_vma=False,
    )
```

profile of v0, /device:TPU:0, one launch (start us, length us, event | category | flops | bytes accessed | tf_op | source)
XLA Modules:
  0.0 87.7 jit_solution(9112376063940538871)
XLA Ops:
  0.7 0.8 reshape.163
  1.4 0.6 gather_fusion
  2.0 0.1 broadcast_compare_fusion
  2.1 0.1 gather.6
  2.2 0.3 convert_reduce_fusion
  2.6 0.9 %select_reduce_fusion = (s32[7,8]{1,0:T(8,128)}, s32[7,8]{1,0:T(8,128)}) fusion(s32[7,32]{1,0:T(8,128)S(1)} %add_select_fusion, s32[7,32]{1,0:T(8,128)S(1)} %get-tuple-element.9, pred[7,32]{1,0:T(8,128)(4,1)S(1)} %fusion.4, s32[7,32]{1,0:T(8,128)S(1)} %get-tuple-element.10, pred[7,32]{1,0:T(8,128)(4,1)S(1)} %broadcast_compare_fusion), kind=kLoop, calls=%fused_computation.6 | loop fusion | flops 14224 | bytes 3584 | tf_op jit(solution)/shard_map/reduce_sum | solution.py:36
  3.5 0.1 eq.93
  3.6 0.3 convert_reduce_fusion.2
  3.9 0.6 convert_element_type.17.msk
  4.5 81.4 %encode_and_grad.1 = (bf16[256,256]{1,0:T(8,128)(2,1)}, bf16[256,256]{1,0:T(8,128)(2,1)}, f32[128,256]{1,0:T(8,128)}) custom-call(s32[7,8]{1,0:T(8,128)} %get-tuple-element.12.tidx, s32[7,8]{1,0:T(8,128)} %get-tuple-element.11.blk, f32[7,2,8]{2,1,0:T(2,128)} %convert_element_type.17.msk, bf16[16,128,256]{2,1,0:T(8,128)(2,1)} %bitcast.8, ...), custom_call_target="tpu_custom_call" | custom-call | tf_op jit(solution)/shard_map/encode_and_grad/pallas_call | solution.py:404
  85.9 1.8 %hand_over.1 = (bf16[256,256]{1,0:T(8,128)(2,1)}, bf16[256,256]{1,0:T(8,128)(2,1)}, f32[128,256]{1,0:T(8,128)}) custom-call(bf16[256,256]{1,0:T(8,128)(2,1)} %get-tuple-element.6.hid_in, bf16[256,256]{1,0:T(8,128)(2,1)} %get-tuple-element.7.ngrad_in, f32[128,256]{1,0:T(8,128)} %get-tuple-element.8.wgrad_in), custom_call_target="tpu_custom_call" | custom-call | tf_op jit(solution)/shard_map/hand_over/pallas_call | solution.py:463
  (8 shorter events, 0.1 us)
where the time goes:
time: 87.9 us; the launch traced here: 87.7 us
  Pallas kernels  83.2 us (95%)
  other arithmetic  2.33 us (3%)
  local copies, waits for them, and re-layouts  1.48 us (2%)
    pallas_call x1, Pallas kernels, shards(): pl.pallas_call(functools.partial(kernel, nb, n, scale, wscale), name='enc...  81.4 us
    pallas_call x1, Pallas kernels, shards(): pl.pallas_call(hand_over, name='hand_over', out_shape=tuple((jax.ShapeDty...  1.78 us

commit v1 on v0

--- a/solution.py
+++ b/solution.py
@@ -9,12 +9,15 @@
 
 R = 3
 CAP = 8
-OFFS = [o for o in range(-R, R + 1) if o != 0]
-SEND_ORDER = [3, -3, 2, -2, 1, -1]
-SERVE_ORDER = [1, -1, 2, -2, 3, -3]
-NCH = 4
-KH = NCH // 2
-CHUNKS = list(range(KH, NCH)) + list(range(KH))
+SEND_ORDER = [3, 2, -2, -1, -3, 1]
+MATE = -1
+PAIRED = {v for v in range(-R, R + 1) if v not in (0, MATE) and -v - 1 not in (0, MATE) and -R <= -v - 1 <= R}
+SERVE_AT = {-3: 2.6, 2: 4.6, -2: 6.6, 1: 7.6, 3: 7.7, -1: 7.8}
+JOIN_AT = {-3: 4.7, 2: 4.8, -2: 7.9, 1: 8.0}
+GATHER_AT = 10.6
+NCH = 8
+NH = 6
+LEAD = NCH // 2
 MESH = pl.DeviceIdType.MESH
 F32 = jnp.float32
 BF16 = jnp.bfloat16
@@ -22,7 +25,7 @@
 
 def tables_for(tile_source, me, nb, tiles, nodes, cb):
     rows = tile_source.reshape(nb, tiles)
-    offs = jnp.arange(-R, R + 1, dtype=jnp.int32)
+    offs = jnp.arange(-R, R + 1, dtype=jnp.int32) * (1 - 2 * (me % 2))
     served = rows[jnp.clip(me - offs, 0, nb - 1)]
     order = jnp.arange(tiles, dtype=jnp.int32)
     before = order[None, :] < order[:, None]
@@ -47,8 +50,9 @@
     hid, ngrad, wgrad,
     cells, emix, cot, dsv, dproj, codes, ls,
     buf, hbuf, hsend, hrecv, wacc, wsend, wrecv, qsend, qrecv, psend, precv, lhs, acc,
+    csend, crecv, hold,
     asend, abuf,
-    zs, zr, hs, hr, hps, hpr, ws, wr, qs, qr, ps, pr, zas, zar,
+    zs, zr, hs, hr, hps, hpr, ws, wr, qs, qr, ps, pr, zas, zar, cs, cr,
 ):
     me = lax.axis_index("band")
     c = lax.axis_index("chan")
@@ -58,8 +62,8 @@
     cb = cot.shape[0]
     krows = cb * blkrows
     cblk = cb // NCH
-    half = krows // 2
-    hblk = cb // 2
+    hrows = NH * cblk * blkrows
+    hblk = NH * cblk
     wrows = wrecv.shape[1]
     per = ch // wrows
 
@@ -77,11 +81,7 @@
 
     def z_sends(f, d, k):
         ok = (pos[f] + 1 < n) & (pos[f] - d >= 0)
-        return ok if k >= KH else ok & (pos[f] + 1 < n - 1)
-
-    def z_recvs(f, d, k):
-        ok = pos[f] - 1 - d >= 0
-        return ok if k >= KH else ok & (pos[f] < n - 1)
+        return ok if k >= NH else ok & (pos[f] + 1 < n - 1)
 
     def z_copy(f, d, k):
         rows = pl.ds(k * cblk, cblk)
@@ -99,24 +99,49 @@
         return rc(src, abuf.at[f, d, t], zas.at[f, d, t], zar.at[f, d, t], {"chan": nxt[f]})
 
     def help_copy(f):
-        return rc(dsv.at[pl.ds(0, half)], hbuf.at[f], hs.at[f], hr.at[f], {"chan": prv[f]})
+        return rc(dsv.at[pl.ds(0, hrows)], hbuf.at[f], hs.at[f], hr.at[f], {"chan": prv[f]})
 
     def part_copy(f, e):
         return rc(hsend.at[f, e], hrecv.at[f, e], hps.at[f, e], hpr.at[f, e], {"chan": nxt[f]})
 
-    def q_copy(o):
-        i = OFFS.index(o)
-        return rc(qsend.at[i], qrecv.at[i], qs.at[i], qr.at[i], {"band": lax.rem(me + o + nb, nb)})
-
-    def p_copy(o):
-        i = OFFS.index(o)
-        return rc(psend.at[i], precv.at[i], ps.at[i], pr.at[i], {"band": lax.rem(me - o + nb, nb)})
-
-    def q_sends(o):
-        return (me + o >= 0) & (me + o < nb)
-
-    def q_recvs(o):
-        return (me - o >= 0) & (me - o < nb)
+    par = lax.rem(me, 2)
+    sign = 1 - 2 * par
+    mate = me + sign
+
+    def turn(u):
+        return u if u % 2 == 0 else -u
+
+    def q_copy(u):
+        v = turn(u)
+        to = lax.rem(me + sign * u + nb, nb)
+        return rc(qsend.at[u + R], qrecv.at[v + R], qs.at[u + R], qr.at[v + R], {"band": to})
+
+    def q_from(v):
+        return rc(qsend.at[v + R], qrecv.at[v + R], qs.at[v + R], qr.at[v + R], {"band": me})
+
+    def c_copy(v):
+        w = -v - 1
+        return rc(csend.at[v + R], crecv.at[w + R], cs.at[v + R], cr.at[w + R], {"band": mate})
+
+    def c_from(v):
+        return rc(csend.at[v + R], crecv.at[v + R], cs.at[v + R], cr.at[v + R], {"band": mate})
+
+    def p_copy(v, t):
+        u = turn(v)
+        to = lax.rem(me - sign * v + nb, nb)
+        return rc(psend.at[v + R, t], precv.at[u + R, t], ps.at[v + R, t], pr.at[u + R, t], {"band": to})
+
+    def p_from(u, t):
+        return rc(psend.at[u + R, t], precv.at[u + R, t], ps.at[u + R, t], pr.at[u + R, t], {"band": me})
+
+    def q_sends(u):
+        return (me + sign * u >= 0) & (me + sign * u < nb)
+
+    def q_recvs(v):
+        return (me - sign * v >= 0) & (me - sign * v < nb)
+
+    def p_kinds(v):
+        return [par] if v in PAIRED else [0, 1]
 
     def w_copy(s):
         rows = pl.ds(pl.multiple_of(s * wrows, wrows), wrows)
@@ -182,31 +207,30 @@
     pl.semaphore_wait(barrier, nb - 1 + beside)
 
     loads["cot"].wait()
-    for k in CHUNKS[:KH]:
+    loads["dsv"].wait()
+
+    def start_own(k):
         for f in range(2):
             @pl.when(z_sends(f, 0, k))
             def _():
                 z_copy(f, 0, k).start()
-    for k in CHUNKS[KH:]:
-        for f in range(2):
-            @pl.when(z_sends(f, 0, k))
-            def _():
-                z_copy(f, 0, k).start()
-
-    loads["codes"].wait()
-    for o in SEND_ORDER:
-        @pl.when(q_sends(o))
-        def _():
-            i = OFFS.index(o)
-            for s in range(CAP):
-                qsend[i, s] = (codes[tidx[o + R, s]] - 32768).astype(jnp.int16)
-            q_copy(o).start()
-
-    loads["dsv"].wait()
+
+    for k in range(LEAD):
+        start_own(k)
     for f in range(2):
         @pl.when(pos[f] == n - 1)
         def _():
             help_copy(f).start()
+    for k in range(LEAD, NCH):
+        start_own(k)
+
+    loads["codes"].wait()
+    for u in SEND_ORDER:
+        @pl.when(q_sends(u))
+        def _():
+            for s in range(CAP):
+                qsend[u + R, s] = (codes[tidx[u + R, s]] - 32768).astype(jnp.int16)
+            q_copy(u).start()
 
     loads["cells"].wait()
 
@@ -227,30 +251,49 @@
             out.append(jnp.dot(lhs[t], jnp.concatenate(rhs, axis=0), preferred_element_type=F32))
         return out
 
-    own = serve(0, lambda s: codes[tidx[R, s]] - 32768)
-    acc[0], acc[1] = own
-
-    w_add(c, wdot(cot[...], dsv[...]), True)
-    w_done(c)
-
-    def answer(o):
-        @pl.when(q_recvs(o))
-        def _():
-            i = OFFS.index(o)
-            q_copy(o).wait_recv()
-            parts = serve(o, lambda s: qrecv[i, s].astype(jnp.int32))
-            psend[i, 0] = parts[0].astype(BF16)
-            psend[i, 1] = parts[1].astype(BF16)
-            p_copy(o).start()
+    def serve_own():
+        own = serve(0, lambda s: codes[tidx[R, s]] - 32768)
+        acc[0], acc[1] = own
+
+    def w_own():
+        w_add(c, wdot(cot[...], dsv[...]), True)
+        w_done(c)
+
+    def answer(v):
+        @pl.when(q_recvs(v))
+        def _():
+            q_from(v).wait_recv()
+            parts = serve(v, lambda s: qrecv[v + R, s].astype(jnp.int32))
+            if v in PAIRED:
+                hold[v + R] = jnp.where(par == 0, parts[0], parts[1])
+                csend[v + R] = jnp.where(par == 0, parts[1], parts[0]).astype(BF16)
+                c_copy(v).start()
+            else:
+                for t in range(2):
+                    psend[v + R, t] = parts[t].astype(BF16)
+                    p_copy(v, t).start()
+
+    def join(v):
+        @pl.when(q_recvs(v))
+        def _():
+            c_from(v).wait_recv()
+            psend[v + R, par] = (hold[v + R] + crecv[v + R].astype(F32)).astype(BF16)
+            p_copy(v, par).start()
 
     def aggregate():
-        for o in SERVE_ORDER:
-            @pl.when(q_sends(o))
+        for v in SERVE_AT:
+            u = turn(v)
+
+            @pl.when(q_sends(u))
             def _():
-                i = OFFS.index(o)
-                p_copy(o).wait_recv()
-                for t in range(2):
-                    acc[t] += precv[i, t].astype(F32)
+                if v in PAIRED:
+                    t = lax.rem(par + u + 2 * R, 2)
+                    p_from(u, t).wait_recv()
+                    acc[t] += precv[u + R, t].astype(F32)
+                else:
+                    for t in range(2):
+                        p_from(u, t).wait_recv()
+                        acc[t] += precv[u + R, t].astype(F32)
         for t in range(2):
             asend[t] = (acc[t] * scale).astype(BF16)
             for f in range(2):
@@ -258,47 +301,86 @@
                 def _():
                     a_copy(f, 0, t).start()
 
-    pending = list(SERVE_ORDER)
-    for d in range(n - 1):
-        for j, k in enumerate(CHUNKS):
-            for f in range(2):
-                @pl.when(z_recvs(f, d, k))
-                def _():
-                    z_copy(f, d, k).wait_recv()
-
-                    if d + 1 < n - 1:
-                        @pl.when(z_sends(f, d + 1, k))
-                        def _():
-                            z_copy(f, d + 1, k).start()
-            for o in pending[:2]:
-                answer(o)
-            pending = pending[2:]
-            if j == KH - 1:
-                for f in range(2):
-                    @pl.when(z_recvs(f, d, NCH - 1))
-                    def _():
-                        w_add(owner(f, d), wdot(buf[f, d, hblk:], dsv[half:]), True)
-                if d == 1:
-                    aggregate()
-            if j == NCH - 1:
-                for f in range(2):
-                    if d == 0:
-                        @pl.when(pos[f] == n - 2)
-                        def _():
-                            help_copy(f).wait_recv()
-                            hsend[f, 0] = wdot(cot[:hblk], hbuf[f]).astype(BF16)
-                            part_copy(f, 0).start()
-
-                    @pl.when(z_recvs(f, d, 0))
-                    def _():
-                        if d + 1 < n - 1:
-                            @pl.when(pos[f] == n - 2)
-                            def _():
-                                hsend[f, d + 1] = wdot(buf[f, d, :hblk], hbuf[f]).astype(BF16)
-                                part_copy(f, d + 1).start()
-
-                        w_add(owner(f, d), wdot(buf[f, d, :hblk], dsv[:half]), False)
-                        w_done(owner(f, d))
+    def take(f, p, d, k):
+        @pl.when(pos[f] == p)
+        def _():
+            z_copy(f, d, k).wait_recv()
+            if p + 1 < n - 1 or (p + 1 == n - 1 and k >= NH):
+                z_copy(f, d + 1, k).start()
+
+    def take_help(f):
+        @pl.when(pos[f] == n - 2)
+        def _():
+            help_copy(f).wait_recv()
+
+    def part_own(f):
+        @pl.when(pos[f] == n - 2)
+        def _():
+            hsend[f, 0] = wdot(cot[:hblk], hbuf[f]).astype(BF16)
+            part_copy(f, 0).start()
+
+    def part_of(f, d):
+        @pl.when(pos[f] == n - 2)
+        def _():
+            hsend[f, d + 1] = wdot(buf[f, d, :hblk], hbuf[f]).astype(BF16)
+            part_copy(f, d + 1).start()
+
+    def w_helped(f, p, d):
+        @pl.when(pos[f] == p)
+        def _():
+            w_add(owner(f, d), wdot(buf[f, d, :hblk], dsv[:hrows]), True)
+
+    def w_rest(f, p, d):
+        @pl.when(pos[f] == p)
+        def _():
+            w_add(owner(f, d), wdot(buf[f, d, hblk:], dsv[hrows:]), p == n - 1)
+            if p < n - 1:
+                w_done(owner(f, d))
+
+    def w_part(f, d):
+        @pl.when(pos[f] == n - 1)
+        def _():
+            part_copy(f, d).wait_recv()
+            w_add(owner(f, d), hrecv[f, d].astype(F32), False)
+            w_done(owner(f, d))
+
+    events = []
+
+    def at(time, fn, *args):
+        events.append((time, len(events), fn, args))
+
+    def arrives(p, d, k):
+        if p == n - 1:
+            return k - NH + 1 if d == 0 else (d - 1) * NCH + k + 2
+        if p == 1:
+            return k + 1 + (NH if k >= LEAD else 0)
+        return d * NCH + k + 1
+
+    at(0.5, serve_own)
+    at(1.5, w_own)
+    for o, time in SERVE_AT.items():
+        at(time, answer, o)
+    for v, time in JOIN_AT.items():
+        at(time, join, v)
+    at(GATHER_AT, aggregate)
+    helped_at = LEAD + NH
+    for f in range(2):
+        at(helped_at + 0.1, take_help, f)
+        at(helped_at + 0.5, part_own, f)
+        for d in range(n - 2):
+            at(max(arrives(n - 2, d, NH - 1), helped_at) + 0.6, part_of, f, d)
+        for p in range(1, n):
+            for d in range(p):
+                for k in range(NH if p == n - 1 else 0, NCH):
+                    at(arrives(p, d, k), take, f, p, d, k)
+                if p < n - 1:
+                    at(arrives(p, d, NH - 1) + 0.7, w_helped, f, p, d)
+                at(arrives(p, d, NCH - 1) + 0.4, w_rest, f, p, d)
+        for d in range(n - 1):
+            known = helped_at if d == 0 else max(arrives(n - 2, d - 1, NH - 1), helped_at)
+            at(max(known + 2.5, arrives(n - 1, d, NCH - 1) + 0.5), w_part, f, d)
+    for _, _, fn, args in sorted(events, key=lambda e: e[:2]):
+        fn(*args)
 
     mixes = (emix, dproj)
     loads["emix"].wait()
@@ -310,14 +392,6 @@
 
     for t in range(2):
         acc[t] = mix(t, c, asend[t])
-
-    for d in range(n - 1):
-        for f in range(2):
-            @pl.when(pos[f] == n - 1)
-            def _():
-                part_copy(f, d).wait_recv()
-                w_add(owner(f, d), hrecv[f, d].astype(F32), False)
-                w_done(owner(f, d))
 
     for d in range(n - 1):
         for t in range(2):
@@ -348,7 +422,7 @@
 
     for f in range(2):
         for d in range(n - 1):
-            for k in CHUNKS:
+            for k in range(NCH):
                 @pl.when(z_sends(f, d, k))
                 def _():
                     z_copy(f, d, k).wait_send()
@@ -364,14 +438,18 @@
         @pl.when(pos[f] == n - 1)
         def _():
             help_copy(f).wait_send()
-    for o in OFFS:
-        @pl.when(q_sends(o))
-        def _():
-            q_copy(o).wait_send()
-
-        @pl.when(q_recvs(o))
-        def _():
-            p_copy(o).wait_send()
+    for u in SEND_ORDER:
+        @pl.when(q_sends(u))
+        def _():
+            q_copy(u).wait_send()
+
+    for v in SERVE_AT:
+        @pl.when(q_recvs(v))
+        def _():
+            for t in p_kinds(v):
+                p_copy(v, t).wait_send()
+            if v in PAIRED:
+                c_copy(v).wait_send()
 
     @pl.loop(0, nb)
     def _(s):
@@ -397,7 +475,7 @@
     scale = (3.0 / (kk * blkn)) ** 0.5 / 128.0
     wscale = float(krows * nb) ** -0.5
     tidx, blk, msk = tables_for(tile_source, me, nb, tiles, nodes, cb)
-    no = len(OFFS)
+    no = 2 * R + 1
     nn = nodes * blkn
     dma = pltpu.SemaphoreType.DMA
     vm = pltpu.VMEM
@@ -422,7 +500,7 @@
             vm((tiles, blkn, blkc), jnp.int32),
             dma((6,)),
             vm((2, n - 1, cb, blkc, ch), BF16),
-            vm((2, krows // 2, ch), BF16),
+            vm((2, krows * NH // NCH, ch), BF16),
             vm((2, n - 1, ch, ch), BF16),
             vm((2, n - 1, ch, ch), BF16),
             vm((width, ch), F32),
@@ -434,6 +512,9 @@
             vm((no, 2, nn, ch), BF16),
             vm((2, nn, CAP * blkc), BF16),
             vm((2, nn, ch), F32),
+            vm((no, nn, ch), BF16),
+            vm((no, nn, ch), BF16),
+            vm((no, nn, ch), F32),
             vm((2, nn, ch), BF16),
             vm((2, n - 1, 2, nn, ch), BF16),
             dma((2, n - 1, NCH)),
@@ -446,10 +527,12 @@
             dma((nb,)),
             dma((no,)),
             dma((no,)),
+            dma((no, 2)),
+            dma((no, 2)),
+            dma((2, n - 1, 2)),
+            dma((2, n - 1, 2)),
             dma((no,)),
             dma((no,)),
-            dma((2, n - 1, 2)),
-            dma((2, n - 1, 2)),
         ],
         compiler_params=pltpu.CompilerParams(
             collective_id=0, has_side_effects=True, vmem_limit_bytes=56 * 1024 * 1024

time: 87.9 us -> 83.5 us (0.950)
  the two profiles are of different devices: /device:TPU:0 before, /device:TPU:1 now
where the time goes in v1:
time: 83.5 us; the launch traced here: 83.4 us
  Pallas kernels  78.8 us (94%)
  other arithmetic  2.33 us (3%)
  local copies, waits for them, and re-layouts  1.48 us (2%)
    pallas_call x1, Pallas kernels, shards(): pl.pallas_call(functools.partial(kernel, nb, n, scale, wscale), name='enc...  77.1 us
    pallas_call x1, Pallas kernels, shards(): pl.pallas_call(hand_over, name='hand_over', out_shape=tuple((jax.ShapeDty...  1.78 us

profile of v1, /device:TPU:1, one launch (start us, length us, event | category | flops | bytes accessed | tf_op | source)
XLA Modules:
  0.0 83.4 jit_solution(7156657597416839205)
XLA Ops:
  0.7 0.8 reshape.166
  1.5 0.6 gather_fusion
  2.0 0.1 broadcast_compare_fusion
  2.1 0.1 gather.6
  2.3 0.3 convert_reduce_fusion
  2.6 0.9 %select_reduce_fusion = (s32[7,8]{1,0:T(8,128)}, s32[7,8]{1,0:T(8,128)}) fusion(s32[7,32]{1,0:T(8,128)S(1)} %add_select_fusion, s32[7,32]{1,0:T(8,128)S(1)} %get-tuple-element.9, pred[7,32]{1,0:T(8,128)(4,1)S(1)} %fusion.4, s32[7,32]{1,0:T(8,128)S(1)} %get-tuple-element.10, pred[7,32]{1,0:T(8,128)(4,1)S(1)} %broadcast_compare_fusion), kind=kLoop, calls=%fused_computation.6 | loop fusion | flops 14224 | bytes 3584 | tf_op jit(solution)/shard_map/reduce_sum | solution.py:39
  3.5 0.1 eq.95
  3.6 0.3 convert_reduce_fusion.2
  3.9 0.6 convert_element_type.17.msk
  4.5 77.1 %encode_and_grad.1 = (bf16[256,256]{1,0:T(8,128)(2,1)}, bf16[256,256]{1,0:T(8,128)(2,1)}, f32[128,256]{1,0:T(8,128)}) custom-call(s32[7,8]{1,0:T(8,128)} %get-tuple-element.12.tidx, s32[7,8]{1,0:T(8,128)} %get-tuple-element.11.blk, f32[7,2,8]{2,1,0:T(2,128)} %convert_element_type.17.msk, bf16[16,128,256]{2,1,0:T(8,128)(2,1)} %bitcast.8, ...), custom_call_target="tpu_custom_call" | custom-call | tf_op jit(solution)/shard_map/encode_and_grad/pallas_call | solution.py:482
  81.6 1.8 %hand_over.1 = (bf16[256,256]{1,0:T(8,128)(2,1)}, bf16[256,256]{1,0:T(8,128)(2,1)}, f32[128,256]{1,0:T(8,128)}) custom-call(bf16[256,256]{1,0:T(8,128)(2,1)} %get-tuple-element.6.hid_in, bf16[256,256]{1,0:T(8,128)(2,1)} %get-tuple-element.7.ngrad_in, f32[128,256]{1,0:T(8,128)} %get-tuple-element.8.wgrad_in), custom_call_target="tpu_custom_call" | custom-call | tf_op jit(solution)/shard_map/hand_over/pallas_call | solution.py:546
  (8 shorter events, 0.1 us)

commit v2 on v1

--- a/solution.py
+++ b/solution.py
@@ -18,37 +18,19 @@
 NCH = 8
 NH = 6
 LEAD = NCH // 2
+AP = 2
+WSUM = 2
 MESH = pl.DeviceIdType.MESH
 F32 = jnp.float32
 BF16 = jnp.bfloat16
 
 
-def tables_for(tile_source, me, nb, tiles, nodes, cb):
-    rows = tile_source.reshape(nb, tiles)
-    offs = jnp.arange(-R, R + 1, dtype=jnp.int32) * (1 - 2 * (me % 2))
-    served = rows[jnp.clip(me - offs, 0, nb - 1)]
-    order = jnp.arange(tiles, dtype=jnp.int32)
-    before = order[None, :] < order[:, None]
-
-    def onehot(sel):
-        rank = jnp.sum((sel[:, None, :] & before[None]).astype(jnp.int32), axis=2)
-        slots = jnp.arange(CAP, dtype=jnp.int32)
-        return (sel[:, :, None] & (rank[:, :, None] == slots)).astype(jnp.int32)
-
-    serve = onehot(served // cb == me)
-    blk = jnp.sum(serve * (served % cb)[:, :, None], axis=1)
-    mask = jnp.sum(serve.reshape(2 * R + 1, nodes, tiles // nodes, CAP), axis=2)
-    mine = rows[me]
-    send = onehot((mine // cb)[None, :] == (me + offs)[:, None])
-    tidx = jnp.sum(send * order[None, :, None], axis=1)
-    return tidx, blk, mask.astype(F32)
-
-
 def kernel(
     nb, n, scale, wscale,
-    tidx, blk, msk, cells_in, embed, emix_in, cot_in, dsv_in, dproj_in, codes_in,
-    hid, ngrad, wgrad,
-    cells, emix, cot, dsv, dproj, codes, ls,
+    src_of, cells_in, embed_in, emix_in, cot_in, dsv_in, dproj_in, codes_in,
+    hid_out, ngrad_out, wgrad_out,
+    hid, ngrad, wgrad, outs,
+    cells, embed, emix, cot, dsv, dproj, codes, ls,
     buf, hbuf, hsend, hrecv, wacc, wsend, wrecv, qsend, qrecv, psend, precv, lhs, acc,
     csend, crecv, hold,
     asend, abuf,
@@ -56,7 +38,8 @@
 ):
     me = lax.axis_index("band")
     c = lax.axis_index("chan")
-    nodes = msk.shape[1]
+    kk = src_of.shape[1]
+    nodes = codes.shape[0] // kk
     blkrows = cells.shape[1]
     ch = embed.shape[1]
     cb = cot.shape[0]
@@ -91,12 +74,12 @@
     def a_sends(f, d):
         return (pos[f] + 1 < n) & (pos[f] - d >= 0)
 
-    def a_recvs(f, d):
-        return pos[f] - 1 - d >= 0
-
-    def a_copy(f, d, t):
-        src = asend.at[t] if d == 0 else abuf.at[f, d - 1, t]
-        return rc(src, abuf.at[f, d, t], zas.at[f, d, t], zar.at[f, d, t], {"chan": nxt[f]})
+    arows = embed.shape[0] // AP
+
+    def a_copy(f, d, t, h):
+        rows = pl.ds(h * arows, arows)
+        src = asend.at[t, rows] if d == 0 else abuf.at[f, d - 1, t, rows]
+        return rc(src, abuf.at[f, d, t, rows], zas.at[f, d, t, h], zar.at[f, d, t, h], {"chan": nxt[f]})
 
     def help_copy(f):
         return rc(dsv.at[pl.ds(0, hrows)], hbuf.at[f], hs.at[f], hr.at[f], {"chan": prv[f]})
@@ -110,6 +93,35 @@
 
     def turn(u):
         return u if u % 2 == 0 else -u
+
+    def picks(band, wanted):
+        low = wanted * cb
+        bits = (max(cb, kk) - 1).bit_length()
+        one = jnp.int32(1)
+        zero = jnp.int32(0)
+        seen, block, place, part = zero, zero, zero, zero
+        unit, flag = one, one
+        for m in range(nodes):
+            for k in range(kk):
+                off = src_of[band * nodes + m, k] - low
+                hit = (off >= 0) & (off < cb)
+                block += jnp.where(hit, off * unit, 0)
+                place += jnp.where(hit, k * unit, 0)
+                part += jnp.where(hit, m * flag, 0)
+                seen += jnp.where(hit, 1, 0)
+                unit = jnp.where(hit, unit * 2**bits, unit)
+                flag = jnp.where(hit, flag * nodes, flag)
+
+        def field(word, s, size):
+            return (word >> (size * s)) & (2**size - 1)
+
+        mbits = (nodes - 1).bit_length()
+        slots = []
+        for s in range(CAP):
+            m = field(part, s, mbits)
+            keeps = [jnp.where((m == i) & (s < seen), 1.0, 0.0) for i in range(nodes)]
+            slots.append((m * kk + field(place, s, bits), field(block, s, bits), keeps))
+        return slots
 
     def q_copy(u):
         v = turn(u)
@@ -184,6 +196,7 @@
                 ("cells", cells_in, cells),
                 ("emix", emix_in, emix),
                 ("dproj", dproj_in, dproj),
+                ("embed", embed_in, embed),
             )
         )
     }
@@ -228,31 +241,31 @@
     for u in SEND_ORDER:
         @pl.when(q_sends(u))
         def _():
-            for s in range(CAP):
-                qsend[u + R, s] = (codes[tidx[u + R, s]] - 32768).astype(jnp.int16)
+            for s, (tile, _, _) in enumerate(picks(me, me + sign * u)):
+                qsend[u + R, s] = (codes[tile] - 32768).astype(jnp.int16)
             q_copy(u).start()
 
     loads["cells"].wait()
 
-    def serve(o, load):
-        for s in range(CAP):
-            word = load(s)
+    def serve(slots, load):
+        for s, (tile, _, keeps) in enumerate(slots):
+            word = load(s, tile)
             cols = pl.ds(s * blkrows, blkrows)
             enc = ((word & 255) - 128).astype(F32)
             dec = (word >> 8).astype(F32)
             for m in range(nodes):
-                keep = msk[o + R, m, s]
+                keep = keeps[m]
                 rows = pl.ds(m * blkrows, blkrows)
                 lhs[0, rows, cols] = (enc * keep).astype(BF16)
                 lhs[1, rows, cols] = (dec * keep).astype(BF16)
         out = []
         for t, src in enumerate((cells, cot)):
-            rhs = [src[blk[o + R, s]] for s in range(CAP)]
+            rhs = [src[block] for _, block, _ in slots]
             out.append(jnp.dot(lhs[t], jnp.concatenate(rhs, axis=0), preferred_element_type=F32))
         return out
 
     def serve_own():
-        own = serve(0, lambda s: codes[tidx[R, s]] - 32768)
+        own = serve(picks(me, me), lambda s, tile: codes[tile] - 32768)
         acc[0], acc[1] = own
 
     def w_own():
@@ -262,8 +275,9 @@
     def answer(v):
         @pl.when(q_recvs(v))
         def _():
+            slots = picks(me - sign * v, me)
             q_from(v).wait_recv()
-            parts = serve(v, lambda s: qrecv[v + R, s].astype(jnp.int32))
+            parts = serve(slots, lambda s, tile: qrecv[v + R, s].astype(jnp.int32))
             if v in PAIRED:
                 hold[v + R] = jnp.where(par == 0, parts[0], parts[1])
                 csend[v + R] = jnp.where(par == 0, parts[1], parts[0]).astype(BF16)
@@ -296,10 +310,56 @@
                         acc[t] += precv[u + R, t].astype(F32)
         for t in range(2):
             asend[t] = (acc[t] * scale).astype(BF16)
-            for f in range(2):
-                @pl.when(a_sends(f, 0))
-                def _():
-                    a_copy(f, 0, t).start()
+        for f in range(2):
+            @pl.when((pos[f] == 0) | (pos[f] == n - 2))
+            def _():
+                a_start(f)
+
+    def a_start(f):
+        for t in range(2):
+            for h in range(AP):
+                a_copy(f, 0, t, h).start()
+
+    def a_own(f, p):
+        @pl.when(pos[f] == p)
+        def _():
+            a_start(f)
+
+    mixes = (emix, dproj)
+
+    def mix(t, own, value):
+        rows = pl.ds(pl.multiple_of(own * ch, ch), ch)
+        return jnp.dot(value, mixes[t][rows, :], preferred_element_type=F32)
+
+    def mix_own():
+        loads["embed"].wait()
+        loads["emix"].wait()
+        loads["dproj"].wait()
+        for t in range(2):
+            acc[t] = mix(t, c, asend[t])
+
+    def a_take(f, p, d, t, h):
+        @pl.when(pos[f] == p)
+        def _():
+            a_copy(f, d, t, h).wait_recv()
+            if p + 1 < n:
+                a_copy(f, d + 1, t, h).start()
+            rows = pl.ds(h * arows, arows)
+            acc[t, rows, :] += mix(t, owner(f, d), abuf[f, d, t, rows, :])
+
+    def finish(t):
+        if t == 0:
+            mixed = acc[0]
+            hid[...] = (embed[...].astype(F32) + mixed / (1.0 + jnp.exp(-mixed))).astype(BF16)
+            stores[0].start()
+        else:
+            ngrad[...] = acc[1].astype(BF16)
+            stores[1].start()
+
+    stores = [
+        pltpu.make_async_copy(src, dst, outs.at[i])
+        for i, (src, dst) in enumerate(((hid, hid_out), (ngrad, ngrad_out), (wgrad, wgrad_out)))
+    ]
 
     def take(f, p, d, k):
         @pl.when(pos[f] == p)
@@ -343,6 +403,68 @@
             part_copy(f, d).wait_recv()
             w_add(owner(f, d), hrecv[f, d].astype(F32), False)
             w_done(owner(f, d))
+
+    def w_sum():
+        total = wacc[pl.ds(pl.multiple_of(me * wrows, wrows), wrows), :]
+        wgrad[...] = total
+
+        @pl.loop(0, nb)
+        def _(s):
+            @pl.when(s != me)
+            def _():
+                w_from(s).wait_recv()
+                wgrad[...] += wrecv[s].astype(F32)
+
+        wgrad[...] = wgrad[...] * wscale
+        stores[2].start()
+
+    def drain_a():
+        for f in range(2):
+            for d in range(n - 1):
+                @pl.when(a_sends(f, d))
+                def _():
+                    for t in range(2):
+                        for h in range(AP):
+                            a_copy(f, d, t, h).wait_send()
+
+    def drain_w():
+        @pl.loop(0, nb)
+        def _(s):
+            @pl.when(s != me)
+            def _():
+                w_copy(s).wait_send()
+
+    def drain_stores():
+        for store in stores:
+            store.wait()
+
+    def drain():
+        for f in range(2):
+            for d in range(n - 1):
+                for k in range(NCH):
+                    @pl.when(z_sends(f, d, k))
+                    def _():
+                        z_copy(f, d, k).wait_send()
+
+                @pl.when(pos[f] == n - 2)
+                def _():
+                    part_copy(f, d).wait_send()
+
+            @pl.when(pos[f] == n - 1)
+            def _():
+                help_copy(f).wait_send()
+        for u in SEND_ORDER:
+            @pl.when(q_sends(u))
+            def _():
+                q_copy(u).wait_send()
+
+        for v in SERVE_AT:
+            @pl.when(q_recvs(v))
+            def _():
+                for t in p_kinds(v):
+                    p_copy(v, t).wait_send()
+                if v in PAIRED:
+                    c_copy(v).wait_send()
 
     events = []
 
@@ -363,6 +485,14 @@
     for v, time in JOIN_AT.items():
         at(time, join, v)
     at(GATHER_AT, aggregate)
+    at(GATHER_AT + 0.3, mix_own)
+    last = 2 * NCH + 2 * n
+
+    def a_arrives(p, d):
+        if p == n - 1:
+            return GATHER_AT + 2.5 if d == 0 else a_arrives(p - 1, d - 1) + 1.5
+        return 2 * NCH + 0.5 + 2 * (d + 1)
+
     helped_at = LEAD + NH
     for f in range(2):
         at(helped_at + 0.1, take_help, f)
@@ -379,83 +509,22 @@
         for d in range(n - 1):
             known = helped_at if d == 0 else max(arrives(n - 2, d - 1, NH - 1), helped_at)
             at(max(known + 2.5, arrives(n - 1, d, NCH - 1) + 0.5), w_part, f, d)
+    for f in range(2):
+        for p in range(1, n):
+            if p + 1 < n - 1:
+                at(max(GATHER_AT, arrives(p, p - 1, NCH - 1)) + 0.35, a_own, f, p)
+            for d in range(p):
+                for t in range(2):
+                    for h in range(AP):
+                        when = a_arrives(p, d) + (t * AP + h) / AP
+                        at(when if p < n - 1 or d < n - 2 else last + t + h / AP, a_take, f, p, d, t, h)
+    at(last + 0.9, finish, 0)
+    at(last + WSUM, w_sum)
+    at(last + 1.9, finish, 1)
+    for i, fn in enumerate((drain, drain_w, drain_a, drain_stores)):
+        at(last + 3 + i, fn)
     for _, _, fn, args in sorted(events, key=lambda e: e[:2]):
         fn(*args)
-
-    mixes = (emix, dproj)
-    loads["emix"].wait()
-    loads["dproj"].wait()
-
-    def mix(t, own, value):
-        rows = pl.ds(pl.multiple_of(own * ch, ch), ch)
-        return jnp.dot(value, mixes[t][rows, :], preferred_element_type=F32)
-
-    for t in range(2):
-        acc[t] = mix(t, c, asend[t])
-
-    for d in range(n - 1):
-        for t in range(2):
-            for f in range(2):
-                @pl.when(a_recvs(f, d))
-                def _():
-                    a_copy(f, d, t).wait_recv()
-                    if d + 1 < n - 1:
-                        @pl.when(a_sends(f, d + 1))
-                        def _():
-                            a_copy(f, d + 1, t).start()
-                    acc[t] += mix(t, owner(f, d), abuf[f, d, t])
-
-    mixed = acc[0]
-    hid[...] = (embed[...].astype(F32) + mixed / (1.0 + jnp.exp(-mixed))).astype(BF16)
-    ngrad[...] = acc[1].astype(BF16)
-
-    wgrad[...] = wacc[pl.ds(pl.multiple_of(me * wrows, wrows), wrows), :]
-
-    @pl.loop(0, nb)
-    def _(s):
-        @pl.when(s != me)
-        def _():
-            w_from(s).wait_recv()
-            wgrad[...] += wrecv[s].astype(F32)
-
-    wgrad[...] = wgrad[...] * wscale
-
-    for f in range(2):
-        for d in range(n - 1):
-            for k in range(NCH):
-                @pl.when(z_sends(f, d, k))
-                def _():
-                    z_copy(f, d, k).wait_send()
-            for t in range(2):
-                @pl.when(a_sends(f, d))
-                def _():
-                    a_copy(f, d, t).wait_send()
-
-            @pl.when(pos[f] == n - 2)
-            def _():
-                part_copy(f, d).wait_send()
-
-        @pl.when(pos[f] == n - 1)
-        def _():
-            help_copy(f).wait_send()
-    for u in SEND_ORDER:
-        @pl.when(q_sends(u))
-        def _():
-            q_copy(u).wait_send()
-
-    for v in SERVE_AT:
-        @pl.when(q_recvs(v))
-        def _():
-            for t in p_kinds(v):
-                p_copy(v, t).wait_send()
-            if v in PAIRED:
-                c_copy(v).wait_send()
-
-    @pl.loop(0, nb)
-    def _(s):
-        @pl.when(s != me)
-        def _():
-            w_copy(s).wait_send()
 
 
 def hand_over(hid_in, ngrad_in, wgrad_in, hid, ngrad, wgrad):
@@ -465,7 +534,6 @@
 
 
 def shards(nb, n, cells_next, node_embed, enc_mix, out_cotangent, decoded_saved, dec_proj, tile_source, tile_codes):
-    me = lax.axis_index("band")
     nodes, kk, blkn, blkc = tile_codes.shape
     tiles = nodes * kk
     krows, ch = out_cotangent.shape
@@ -474,7 +542,6 @@
     wrows = width // nb
     scale = (3.0 / (kk * blkn)) ** 0.5 / 128.0
     wscale = float(krows * nb) ** -0.5
-    tidx, blk, msk = tables_for(tile_source, me, nb, tiles, nodes, cb)
     no = 2 * R + 1
     nn = nodes * blkn
     dma = pltpu.SemaphoreType.DMA
@@ -487,18 +554,21 @@
             jax.ShapeDtypeStruct((nn, ch), BF16),
             jax.ShapeDtypeStruct((wrows, ch), F32),
         ),
-        in_specs=[pl.BlockSpec(memory_space=pltpu.SMEM)] * 3
-        + [pl.BlockSpec(memory_space=pl.ANY), pl.BlockSpec(memory_space=vm)]
-        + [pl.BlockSpec(memory_space=pl.ANY)] * 5,
-        out_specs=[pl.BlockSpec(memory_space=vm)] * 3,
+        in_specs=[pl.BlockSpec(memory_space=pltpu.SMEM)] + [pl.BlockSpec(memory_space=pl.ANY)] * 7,
+        out_specs=[pl.BlockSpec(memory_space=pl.ANY)] * 3,
         scratch_shapes=[
+            vm((nn, ch), BF16),
+            vm((nn, ch), BF16),
+            vm((wrows, ch), F32),
+            dma((3,)),
             vm((cb, blkc, ch), BF16),
+            vm((nn, ch), BF16),
             vm((width, ch), BF16),
             vm((cb, blkc, ch), BF16),
             vm((krows, ch), BF16),
             vm((width, ch), BF16),
             vm((tiles, blkn, blkc), jnp.int32),
-            dma((6,)),
+            dma((7,)),
             vm((2, n - 1, cb, blkc, ch), BF16),
             vm((2, krows * NH // NCH, ch), BF16),
             vm((2, n - 1, ch, ch), BF16),
@@ -529,8 +599,8 @@
             dma((no,)),
             dma((no, 2)),
             dma((no, 2)),
-            dma((2, n - 1, 2)),
-            dma((2, n - 1, 2)),
+            dma((2, n - 1, 2, AP)),
+            dma((2, n - 1, 2, AP)),
             dma((no,)),
             dma((no,)),
         ],
@@ -538,7 +608,7 @@
             collective_id=0, has_side_effects=True, vmem_limit_bytes=56 * 1024 * 1024
         ),
     )(
-        tidx, blk, msk,
+        tile_source,
         cells_next.reshape(cb, blkc, ch), node_embed, enc_mix,
         out_cotangent.reshape(cb, blkc, ch), decoded_saved, dec_proj,
         tile_codes.reshape(tiles, blkn, blkc),

time: 83.5 us -> 76.9 us (0.921)
  the two profiles are of different devices: /device:TPU:1 before, /device:TPU:0 now
where the time goes in v2:
time: 76.9 us; the launch traced here: 75.5 us
  Pallas kernels  74.8 us (97%)
    pallas_call x1, Pallas kernels, shards(): pl.pallas_call(functools.partial(kernel, nb, n, scale, wscale), name='enc...  73 us
    pallas_call x1, Pallas kernels, shards(): pl.pallas_call(hand_over, name='hand_over', out_shape=tuple((jax.ShapeDty...  1.78 us

profile of v2, /device:TPU:0, one launch (start us, length us, event | category | flops | bytes accessed | tf_op | source)
XLA Modules:
  0.0 75.5 jit_solution(1564790443785056710)
XLA Ops:
  0.6 73.0 %encode_and_grad.1 = (bf16[256,256]{1,0:T(8,128)(2,1)}, bf16[256,256]{1,0:T(8,128)(2,1)}, f32[128,256]{1,0:T(8,128)}) custom-call(s32[16,16]{1,0:T(8,128)} %src_of.1, bf16[16,128,256]{2,1,0:T(8,128)(2,1)} %bitcast.4, bf16[256,256]{1,0:T(8,128)(2,1)} %embed_in.1, bf16[1024,256]{1,0:T(8,128)(2,1)} %emix_in.1, bf16[16,128,256]{2,1,0:T(8,128)(2,1)} %bitcast.5, ...), custom_call_target="tpu_custom_call" | custom-call | tf_op jit(solution)/shard_map/encode_and_grad/pallas_call | solution.py:549
  73.7 1.8 %hand_over.1 = (bf16[256,256]{1,0:T(8,128)(2,1)}, bf16[256,256]{1,0:T(8,128)(2,1)}, f32[128,256]{1,0:T(8,128)}) custom-call(bf16[256,256]{1,0:T(8,128)(2,1)} %get-tuple-element.6.hid_in, bf16[256,256]{1,0:T(8,128)(2,1)} %get-tuple-element.7.ngrad_in, f32[128,256]{1,0:T(8,128)} %get-tuple-element.8.wgrad_in), custom_call_target="tpu_custom_call" | custom-call | tf_op jit(solution)/shard_map/hand_over/pallas_call | solution.py:616

commit v3 on v2

--- a/solution.py
+++ b/solution.py
@@ -14,10 +14,10 @@
 PAIRED = {v for v in range(-R, R + 1) if v not in (0, MATE) and -v - 1 not in (0, MATE) and -R <= -v - 1 <= R}
 SERVE_AT = {-3: 2.6, 2: 4.6, -2: 6.6, 1: 7.6, 3: 7.7, -1: 7.8}
 JOIN_AT = {-3: 4.7, 2: 4.8, -2: 7.9, 1: 8.0}
-GATHER_AT = 10.6
+GATHER_AT = 12.3
 NCH = 8
 NH = 6
-LEAD = NCH // 2
+LEAD = 4
 AP = 2
 WSUM = 2
 MESH = pl.DeviceIdType.MESH
@@ -66,10 +66,23 @@
         ok = (pos[f] + 1 < n) & (pos[f] - d >= 0)
         return ok if k >= NH else ok & (pos[f] + 1 < n - 1)
 
+    def slot_at(f, d, ahead):
+        return d if f == 0 else d + c - ahead
+
     def z_copy(f, d, k):
         rows = pl.ds(k * cblk, cblk)
         src = cot.at[rows] if d == 0 else buf.at[f, d - 1, rows]
-        return rc(src, buf.at[f, d, rows], zs.at[f, d, k], zr.at[f, d, k], {"chan": nxt[f]})
+        return rc(src, buf.at[f, d, rows], zs.at[f, d], zr.at[slot_at(f, d, 1), k], {"chan": nxt[f]})
+
+    def z_from(f, d, k):
+        rows = pl.ds(k * cblk, cblk)
+        dst = buf.at[f, d, rows]
+        return rc(dst, dst, zs.at[f, d], zr.at[slot_at(f, d, 0), k], {"chan": nxt[f]})
+
+    def z_sent(f, d, first):
+        rows = pl.ds(first * cblk, cb - first * cblk)
+        dst = buf.at[f, d, rows]
+        return rc(dst, dst, zs.at[f, d], zr.at[0, 0], {"chan": nxt[f]})
 
     def a_sends(f, d):
         return (pos[f] + 1 < n) & (pos[f] - d >= 0)
@@ -79,7 +92,15 @@
     def a_copy(f, d, t, h):
         rows = pl.ds(h * arows, arows)
         src = asend.at[t, rows] if d == 0 else abuf.at[f, d - 1, t, rows]
-        return rc(src, abuf.at[f, d, t, rows], zas.at[f, d, t, h], zar.at[f, d, t, h], {"chan": nxt[f]})
+        return rc(src, abuf.at[f, d, t, rows], zas.at[f, d], zar.at[slot_at(f, d, 1), t, h], {"chan": nxt[f]})
+
+    def a_from(f, d, t, h):
+        dst = abuf.at[f, d, t, pl.ds(h * arows, arows)]
+        return rc(dst, dst, zas.at[f, d], zar.at[slot_at(f, d, 0), t, h], {"chan": nxt[f]})
+
+    def a_sent(f, d):
+        dst = abuf.at[f, d]
+        return rc(dst, dst, zas.at[f, d], zar.at[0, 0, 0], {"chan": nxt[f]})
 
     def help_copy(f):
         return rc(dsv.at[pl.ds(0, hrows)], hbuf.at[f], hs.at[f], hr.at[f], {"chan": prv[f]})
@@ -141,10 +162,14 @@
     def p_copy(v, t):
         u = turn(v)
         to = lax.rem(me - sign * v + nb, nb)
-        return rc(psend.at[v + R, t], precv.at[u + R, t], ps.at[v + R, t], pr.at[u + R, t], {"band": to})
+        return rc(psend.at[v + R, t], precv.at[u + R, t], ps.at[v + R], pr.at[u + R, t], {"band": to})
+
+    def p_sent(v):
+        src = psend.at[v + R, 0] if v in PAIRED else psend.at[v + R]
+        return rc(src, src, ps.at[v + R], ps.at[v + R], {"band": me})
 
     def p_from(u, t):
-        return rc(psend.at[u + R, t], precv.at[u + R, t], ps.at[u + R, t], pr.at[u + R, t], {"band": me})
+        return rc(psend.at[u + R, t], precv.at[u + R, t], ps.at[u + R], pr.at[u + R, t], {"band": me})
 
     def q_sends(u):
         return (me + sign * u >= 0) & (me + sign * u < nb)
@@ -152,16 +177,17 @@
     def q_recvs(v):
         return (me - sign * v >= 0) & (me - sign * v < nb)
 
-    def p_kinds(v):
-        return [par] if v in PAIRED else [0, 1]
-
     def w_copy(s):
         rows = pl.ds(pl.multiple_of(s * wrows, wrows), wrows)
-        return rc(wsend.at[rows], wrecv.at[me], ws.at[s], wr.at[me], {"band": s})
-
-    def w_from(s):
-        rows = pl.ds(pl.multiple_of(s * wrows, wrows), wrows)
-        return rc(wsend.at[rows], wrecv.at[s], ws.at[s], wr.at[s], {"band": s})
+        return rc(wsend.at[rows], wrecv.at[me], ws.at[0], wr.at[0], {"band": s})
+
+    def w_all():
+        rows = wsend.at[pl.ds(0, (nb - 1) * wrows)]
+        return rc(rows, rows, ws.at[0], ws.at[0], {"band": me})
+
+    def w_got():
+        blocks = wrecv.at[pl.ds(0, nb - 1)]
+        return rc(blocks, blocks, wr.at[0], wr.at[0], {"band": me})
 
     def wdot(a, b):
         a = a.reshape(-1, ch)
@@ -341,7 +367,7 @@
     def a_take(f, p, d, t, h):
         @pl.when(pos[f] == p)
         def _():
-            a_copy(f, d, t, h).wait_recv()
+            a_from(f, d, t, h).wait_recv()
             if p + 1 < n:
                 a_copy(f, d + 1, t, h).start()
             rows = pl.ds(h * arows, arows)
@@ -364,7 +390,7 @@
     def take(f, p, d, k):
         @pl.when(pos[f] == p)
         def _():
-            z_copy(f, d, k).wait_recv()
+            z_from(f, d, k).wait_recv()
             if p + 1 < n - 1 or (p + 1 == n - 1 and k >= NH):
                 z_copy(f, d + 1, k).start()
 
@@ -405,14 +431,13 @@
             w_done(owner(f, d))
 
     def w_sum():
-        total = wacc[pl.ds(pl.multiple_of(me * wrows, wrows), wrows), :]
-        wgrad[...] = total
+        w_got().wait_recv()
+        wgrad[...] = wacc[pl.ds(pl.multiple_of(me * wrows, wrows), wrows), :]
 
         @pl.loop(0, nb)
         def _(s):
             @pl.when(s != me)
             def _():
-                w_from(s).wait_recv()
                 wgrad[...] += wrecv[s].astype(F32)
 
         wgrad[...] = wgrad[...] * wscale
@@ -423,16 +448,10 @@
             for d in range(n - 1):
                 @pl.when(a_sends(f, d))
                 def _():
-                    for t in range(2):
-                        for h in range(AP):
-                            a_copy(f, d, t, h).wait_send()
+                    a_sent(f, d).wait_send()
 
     def drain_w():
-        @pl.loop(0, nb)
-        def _(s):
-            @pl.when(s != me)
-            def _():
-                w_copy(s).wait_send()
+        w_all().wait_send()
 
     def drain_stores():
         for store in stores:
@@ -441,10 +460,13 @@
     def drain():
         for f in range(2):
             for d in range(n - 1):
-                for k in range(NCH):
-                    @pl.when(z_sends(f, d, k))
-                    def _():
-                        z_copy(f, d, k).wait_send()
+                @pl.when(z_sends(f, d, NCH - 1) & (pos[f] + 1 < n - 1))
+                def _():
+                    z_sent(f, d, 0).wait_send()
+
+                @pl.when(z_sends(f, d, NCH - 1) & (pos[f] + 1 == n - 1))
+                def _():
+                    z_sent(f, d, NH).wait_send()
 
                 @pl.when(pos[f] == n - 2)
                 def _():
@@ -461,8 +483,7 @@
         for v in SERVE_AT:
             @pl.when(q_recvs(v))
             def _():
-                for t in p_kinds(v):
-                    p_copy(v, t).wait_send()
+                p_sent(v).wait_send()
                 if v in PAIRED:
                     c_copy(v).wait_send()
 
@@ -587,20 +608,20 @@
             vm((no, nn, ch), F32),
             vm((2, nn, ch), BF16),
             vm((2, n - 1, 2, nn, ch), BF16),
-            dma((2, n - 1, NCH)),
-            dma((2, n - 1, NCH)),
+            dma((2, n - 1)),
+            dma((n - 1, NCH)),
             dma((2,)),
             dma((2,)),
             dma((2, n - 1)),
             dma((2, n - 1)),
-            dma((nb,)),
-            dma((nb,)),
+            dma((1,)),
+            dma((1,)),
+            dma((no,)),
             dma((no,)),
             dma((no,)),
             dma((no, 2)),
-            dma((no, 2)),
-            dma((2, n - 1, 2, AP)),
-            dma((2, n - 1, 2, AP)),
+            dma((2, n - 1)),
+            dma((n - 1, 2, AP)),
             dma((no,)),
             dma((no,)),
         ],

time: 76.9 us -> 73.7 us (0.958); the launches traced: 75.5 us -> 73.6 us
  Pallas kernels: 74.8 us -> 72.9 us
    pallas_call x1, Pallas kernels: 73 us -> 71.1 us  [shards(): pl.pallas_call(functools.partial(kernel, nb, n, scale, wscale), name='enc...]
where the time goes in v3:
time: 73.7 us; the launch traced here: 73.6 us
  Pallas kernels  72.9 us (99%)
    pallas_call x1, Pallas kernels, shards(): pl.pallas_call(functools.partial(kernel, nb, n, scale, wscale), name='enc...  71.1 us
    pallas_call x1, Pallas kernels, shards(): pl.pallas_call(hand_over, name='hand_over', out_shape=tuple((jax.ShapeDty...  1.78 us

profile of v3, /device:TPU:0, one launch (start us, length us, event | category | flops | bytes accessed | tf_op | source)
XLA Modules:
  0.0 73.6 jit_solution(11006551402329131985)
XLA Ops:
  0.6 71.1 %encode_and_grad.1 = (bf16[256,256]{1,0:T(8,128)(2,1)}, bf16[256,256]{1,0:T(8,128)(2,1)}, f32[128,256]{1,0:T(8,128)}) custom-call(s32[16,16]{1,0:T(8,128)} %src_of.1, bf16[16,128,256]{2,1,0:T(8,128)(2,1)} %bitcast.4, bf16[256,256]{1,0:T(8,128)(2,1)} %embed_in.1, bf16[1024,256]{1,0:T(8,128)(2,1)} %emix_in.1, bf16[16,128,256]{2,1,0:T(8,128)(2,1)} %bitcast.5, ...), custom_call_target="tpu_custom_call" | custom-call | tf_op jit(solution)/shard_map/encode_and_grad/pallas_call | solution.py:570
  71.8 1.8 %hand_over.1 = (bf16[256,256]{1,0:T(8,128)(2,1)}, bf16[256,256]{1,0:T(8,128)(2,1)}, f32[128,256]{1,0:T(8,128)}) custom-call(bf16[256,256]{1,0:T(8,128)(2,1)} %get-tuple-element.6.hid_in, bf16[256,256]{1,0:T(8,128)(2,1)} %get-tuple-element.7.ngrad_in, f32[128,256]{1,0:T(8,128)} %get-tuple-element.8.wgrad_in), custom_call_target="tpu_custom_call" | custom-call | tf_op jit(solution)/shard_map/hand_over/pallas_call | solution.py:637

commit v4 on v3

--- a/solution.py
+++ b/solution.py
@@ -27,10 +27,10 @@
 
 def kernel(
     nb, n, scale, wscale,
-    src_of, cells_in, embed_in, emix_in, cot_in, dsv_in, dproj_in, codes_in,
+    src_in, cells_in, embed_in, emix_in, cot_in, dsv_in, dproj_in, codes_in,
     hid_out, ngrad_out, wgrad_out,
     hid, ngrad, wgrad, outs,
-    cells, embed, emix, cot, dsv, dproj, codes, ls,
+    src_of, cells, embed, emix, cot, dsv, dproj, codes, ls,
     buf, hbuf, hsend, hrecv, wacc, wsend, wrecv, qsend, qrecv, psend, precv, lhs, acc,
     csend, crecv, hold,
     asend, abuf,
@@ -223,6 +223,7 @@
                 ("emix", emix_in, emix),
                 ("dproj", dproj_in, dproj),
                 ("embed", embed_in, embed),
+                ("src", src_in, src_of),
             )
         )
     }
@@ -263,6 +264,7 @@
     for k in range(LEAD, NCH):
         start_own(k)
 
+    loads["src"].wait()
     loads["codes"].wait()
     for u in SEND_ORDER:
         @pl.when(q_sends(u))
@@ -575,13 +577,14 @@
             jax.ShapeDtypeStruct((nn, ch), BF16),
             jax.ShapeDtypeStruct((wrows, ch), F32),
         ),
-        in_specs=[pl.BlockSpec(memory_space=pltpu.SMEM)] + [pl.BlockSpec(memory_space=pl.ANY)] * 7,
+        in_specs=[pl.BlockSpec(memory_space=pl.ANY)] * 8,
         out_specs=[pl.BlockSpec(memory_space=pl.ANY)] * 3,
         scratch_shapes=[
             vm((nn, ch), BF16),
             vm((nn, ch), BF16),
             vm((wrows, ch), F32),
             dma((3,)),
+            pltpu.SMEM(tile_source.shape, jnp.int32),
             vm((cb, blkc, ch), BF16),
             vm((nn, ch), BF16),
             vm((width, ch), BF16),
@@ -589,7 +592,7 @@
             vm((krows, ch), BF16),
             vm((width, ch), BF16),
             vm((tiles, blkn, blkc), jnp.int32),
-            dma((7,)),
+            dma((8,)),
             vm((2, n - 1, cb, blkc, ch), BF16),
             vm((2, krows * NH // NCH, ch), BF16),
             vm((2, n - 1, ch, ch), BF16),

time: 73.7 us -> 73.1 us (level)
  no operation moved by 1% of the time
where the time goes in v4:
time: 73.1 us; the launch traced here: 72.9 us
  Pallas kernels  72.3 us (99%)
    pallas_call x1, Pallas kernels, shards(): pl.pallas_call(functools.partial(kernel, nb, n, scale, wscale), name='enc...  70.5 us
    pallas_call x1, Pallas kernels, shards(): pl.pallas_call(hand_over, name='hand_over', out_shape=tuple((jax.ShapeDty...  1.78 us

profile of v4, /device:TPU:0, one launch (start us, length us, event | category | flops | bytes accessed | tf_op | source)
XLA Modules:
  0.0 72.9 jit_solution(16684462219165201765)
XLA Ops:
  0.6 70.5 %encode_and_grad.1 = (bf16[256,256]{1,0:T(8,128)(2,1)}, bf16[256,256]{1,0:T(8,128)(2,1)}, f32[128,256]{1,0:T(8,128)}) custom-call(s32[16,16]{1,0:T(8,128)} %src_in.1, bf16[16,128,256]{2,1,0:T(8,128)(2,1)} %bitcast.4, bf16[256,256]{1,0:T(8,128)(2,1)} %embed_in.1, bf16[1024,256]{1,0:T(8,128)(2,1)} %emix_in.1, bf16[16,128,256]{2,1,0:T(8,128)(2,1)} %bitcast.5, ...), custom_call_target="tpu_custom_call" | custom-call | tf_op jit(solution)/shard_map/encode_and_grad/pallas_call | solution.py:572
  71.1 1.8 %hand_over.1 = (bf16[256,256]{1,0:T(8,128)(2,1)}, bf16[256,256]{1,0:T(8,128)(2,1)}, f32[128,256]{1,0:T(8,128)}) custom-call(bf16[256,256]{1,0:T(8,128)(2,1)} %get-tuple-element.6.hid_in, bf16[256,256]{1,0:T(8,128)(2,1)} %get-tuple-element.7.ngrad_in, f32[128,256]{1,0:T(8,128)} %get-tuple-element.8.wgrad_in), custom_call_target="tpu_custom_call" | custom-call | tf_op jit(solution)/shard_map/hand_over/pallas_call | solution.py:640
